TPU v7x, 256 devices: a whole 4x4x8 slice. The times are simulated.
256 devices in a mesh: ex: 8 (over z), ctx: 32 (over x, y, core).
Axes of the slice: x: 4, y: 4, z: 8, core: 2. Of those that a mesh axis runs over, the one named last changes fastest.
Arguments:
- stream: bfloat16 [8, 256, 32768], P('ex', None, 'ctx'), may hold values from -6 to 6
- cotangent: bfloat16 [8, 256, 32768], P('ex', None, 'ctx'), may hold values from -6 to 6
- base_ids: int32 [8, 32768], P('ex', 'ctx'), may hold values from 0 to 4
- clip_bound: int32 [8], P('ex'), may hold values from 1 to 4
- w_value: bfloat16 [256, 256], replicated, may hold values from -2 to 2
- w_gate: bfloat16 [256, 256], replicated, may hold values from -0.375 to 0.375
- filter_taps: float32 [256, 32768], P('ctx', 'ex'), may hold values from -0.03125 to 0.03125
- filter_bias: float32 [256], P('ctx'), may hold values from 0.1 to 1.9
Outputs:
- input_grad: bfloat16 [8, 256, 32768], P('ex', None, 'ctx')
- filter_grad: float32 [256, 32768], P('ctx', 'ex')
All inputs are finite; a program needn't handle non-finite values.
Results may differ from a plain program's by a relative error of at most 0.015.
Values may be sent and summed in bfloat16 or wider, within the bound.
No kernel may reach another device: no remote copies, remote signals or barrier semaphores. Data moves between devices by JAX's collectives and lax.ppermute only.
A program may use at most 128 MiB of HBM per device.

v0:
```python
import math
import jax
import jax.numpy as jnp
from jax import lax
from jax.sharding import PartitionSpec as P

RADIX = 128
unknown_base = 4
norm_eps = 1e-06


def joined_along(parts, dim):
    lengths = list(parts.shape[1:])
    lengths[dim] *= parts.shape[0]
    return jnp.moveaxis(parts, 0, dim).reshape(lengths)


def from_everyone(x, axis):
    copies = jnp.broadcast_to(x, (lax.axis_size(axis), *x.shape))
    return lax.all_to_all(copies, axis, split_axis=0, concat_axis=0, tiled=True)


def gathered_copies(x, axis, dim):
    return joined_along(from_everyone(x, axis), dim)


def over_copies(x, axis):
    return from_everyone(x, axis).sum(axis=0)


def cut_along(x, dim, size):
    before, after = (x.shape[:dim], x.shape[dim + 1 :])
    return jnp.moveaxis(x.reshape(*before, size, -1, *after), dim, 0)


def sum_at_owner(x, axis, dim):
    size = lax.axis_size(axis)
    parts = lax.all_to_all(cut_along(x, dim, size), axis, 0, 0, tiled=True)
    return jnp.sum(parts.astype(jnp.float32), axis=0)


def dft_table(order):
    indices = jnp.arange(order, dtype=jnp.int32)
    phase_angle = (indices[:, None] * indices[None, :] % order).astype(jnp.float32) * (
        2.0 * math.pi / order
    )
    return (jnp.cos(phase_angle), jnp.sin(phase_angle))


def twiddle_table(outer, inner):
    whole = outer * inner
    outer_idx = jnp.arange(outer, dtype=jnp.int32)
    inner_idx = jnp.arange(inner, dtype=jnp.int32)
    phase_angle = (outer_idx[:, None] * inner_idx[None, :] % whole).astype(jnp.float32) * (
        2.0 * math.pi / whole
    )
    return (jnp.cos(phase_angle), jnp.sin(phase_angle))


def first_section(signal, cos_long, sin_long, first_block, radix_size):
    channels = signal.shape[0]
    number_blocks = signal.shape[1] // radix_size
    shaped = signal.reshape(channels, number_blocks, radix_size)
    cos_rows = lax.dynamic_slice_in_dim(cos_long, first_block, number_blocks, 0)
    sin_rows = lax.dynamic_slice_in_dim(sin_long, first_block, number_blocks, 0)
    real_part = jnp.einsum("cbk,bf->ckf", shaped, cos_rows)
    imag_part = -jnp.einsum("cbk,bf->ckf", shaped, sin_rows)
    return (real_part, imag_part)


def second_section(real_part, imag_part, tables):
    cos_long, sin_long, cos_short, sin_short, cos_twist, sin_twist = tables
    twist_real = real_part * cos_twist + imag_part * sin_twist
    twist_imag = imag_part * cos_twist - real_part * sin_twist
    out_real = jnp.einsum("fk,ckg->cfg", cos_short, twist_real)
    out_real = out_real + jnp.einsum("fk,ckg->cfg", sin_short, twist_imag)
    out_imag = jnp.einsum("fk,ckg->cfg", cos_short, twist_imag)
    out_imag = out_imag - jnp.einsum("fk,ckg->cfg", sin_short, twist_real)
    return (out_real, out_imag)


def forward_full(signal, tables, radix_size):
    real_part, imag_part = first_section(signal, tables[0], tables[1], 0, radix_size)
    return second_section(real_part, imag_part, tables)


def inverse_half(real_part, imag_part, tables, half_blocks):
    cos_long, sin_long, cos_short, sin_short, cos_twist, sin_twist = tables
    mid_real = jnp.einsum("tf,cfg->ctg", cos_short, real_part)
    mid_real = mid_real - jnp.einsum("tf,cfg->ctg", sin_short, imag_part)
    mid_imag = jnp.einsum("tf,cfg->ctg", cos_short, imag_part)
    mid_imag = mid_imag + jnp.einsum("tf,cfg->ctg", sin_short, real_part)
    twist_real = mid_real * cos_twist - mid_imag * sin_twist
    twist_imag = mid_real * sin_twist + mid_imag * cos_twist
    cos_cols = cos_long[:, :half_blocks]
    sin_cols = sin_long[:, :half_blocks]
    outputs = jnp.einsum("ckg,gt->ctk", twist_real, cos_cols)
    outputs = outputs - jnp.einsum("ckg,gt->ctk", twist_imag, sin_cols)
    whole = cos_short.shape[0] * cos_long.shape[0]
    return outputs.reshape(outputs.shape[0], -1) * (1.0 / whole)


def on_device(stream, cotangent, base_ids, clip_bound, w_value, w_gate, filter_taps, filter_bias):
    tokens_in = stream[0]
    value_tok = jnp.dot(w_value, tokens_in, preferred_element_type=jnp.float32).astype(jnp.bfloat16)
    gate_tok = jnp.dot(w_gate, tokens_in, preferred_element_type=jnp.float32).astype(jnp.bfloat16)
    keep_mask = (base_ids[0] != unknown_base).astype(jnp.float32)
    cot_tok = cotangent[0].astype(jnp.float32) * keep_mask[None, :]
    signal_tok = (gate_tok.astype(jnp.float32) * cot_tok).astype(jnp.bfloat16)
    radix_size = RADIX
    seq_len = tokens_in.shape[1] * lax.axis_size("ctx")
    long_order = 2 * seq_len // radix_size
    half_blocks = long_order // 2
    cos_long, sin_long = dft_table(long_order)
    cos_short, sin_short = dft_table(radix_size)
    cos_twist, sin_twist = twiddle_table(radix_size, long_order)
    tables = (cos_long, sin_long, cos_short, sin_short, cos_twist, sin_twist)
    channels = filter_taps.shape[0]
    zeros_spec = jnp.zeros((channels, radix_size, long_order), jnp.float32)
    first_block = jnp.int32(0) // radix_size
    real_part, imag_part = first_section(
        gathered_copies(filter_taps.astype(jnp.bfloat16), "ex", 1).astype(filter_taps.dtype),
        cos_long,
        sin_long,
        first_block,
        radix_size,
    )
    taps_real = zeros_spec + real_part
    taps_imag = zeros_spec + imag_part
    filt_real, filt_imag = second_section(taps_real, taps_imag, tables)
    value_ch, signal_ch = (
        lax.all_to_all(value_tok, "ctx", split_axis=0, concat_axis=1, tiled=True),
        lax.all_to_all(signal_tok, "ctx", split_axis=0, concat_axis=1, tiled=True),
    )
    value_wide = value_ch.astype(jnp.float32)
    signal_wide = signal_ch.astype(jnp.float32)
    val_real, val_imag = forward_full(value_wide, tables, radix_size)
    grad_real, grad_imag = forward_full(signal_wide, tables, radix_size)
    bias_col = filter_bias[:, None]
    conv_out = inverse_half(
        filt_real * val_real - filt_imag * val_imag,
        filt_real * val_imag + filt_imag * val_real,
        tables,
        half_blocks,
    )
    conv_state = (conv_out + bias_col * value_wide).astype(jnp.bfloat16)
    back_out = inverse_half(
        filt_real * grad_real + filt_imag * grad_imag,
        filt_real * grad_imag - filt_imag * grad_real,
        tables,
        half_blocks,
    )
    value_grad_ch = (back_out + bias_col * signal_wide).astype(jnp.bfloat16)
    taps_grad = inverse_half(
        grad_real * val_real + grad_imag * val_imag,
        grad_imag * val_real - grad_real * val_imag,
        tables,
        half_blocks,
    )
    value_grad_tok, state_tok = (
        lax.all_to_all(value_grad_ch, "ctx", split_axis=1, concat_axis=0, tiled=True),
        lax.all_to_all(conv_state, "ctx", split_axis=1, concat_axis=0, tiled=True),
    )
    gate_grad_tok = (state_tok.astype(jnp.float32) * cot_tok).astype(jnp.bfloat16)
    input_grad = jnp.dot(w_value.T, value_grad_tok, preferred_element_type=jnp.float32)
    input_grad = input_grad + jnp.dot(w_gate.T, gate_grad_tok, preferred_element_type=jnp.float32)
    input_grad = input_grad.astype(jnp.bfloat16)[None]
    width = w_value.shape[0]
    entries = float(seq_len * width)
    square_sum = jnp.sum(taps_grad * taps_grad)
    bound_value = clip_bound[0].astype(jnp.float32)
    grand_total = over_copies(square_sum, "ctx")
    factor = jnp.minimum(1.0, bound_value / jnp.sqrt(grand_total / entries + norm_eps))
    filter_grad = sum_at_owner((factor * taps_grad).astype(jnp.bfloat16), "ex", 1)
    return (input_grad, filter_grad)


def solution(mesh):
    in_specs = (
        P("ex", None, "ctx"),
        P("ex", None, "ctx"),
        P("ex", "ctx"),
        P("ex"),
        P(),
        P(),
        P("ctx", "ex"),
        P("ctx"),
    )
    out_specs = (P("ex", None, "ctx"), P("ctx", "ex"))
    return jax.shard_map(
        on_device, mesh=mesh, in_specs=in_specs, out_specs=out_specs, check_vma=False
    )
```

profile of v0, /device:TPU:1, one launch (start us, length us, event | category | flops | bytes accessed | tf_op | source)
XLA Modules:
  0.0 182.3 jit_solution(5698253643525853579)
XLA Ops:
  1.7 2.3 %fusion.88 = bf16[32,8,1024]{2,1,0:T(8,128)(2,1)} fusion(bf16[256,256]{1,0:T(8,128)(2,1)} %param.13, bf16[1,256,1024]{2,1,0:T(8,128)(2,1)} %param.9, bf16[1,256,1024]{2,1,0:T(8,128)(2,1)S(1)} %copy-done, f32[1024]{0:T(1024)S(1)} %bitcast.287), kind=kOutput, calls=%fused_computation.94 | convolution fusion | flops 135790592 | bytes 1708032 | tf_op jit(solution)/shard_map/dot_general | solution.py:106
  4.0 8.6 %all-to-all-start.1 = ((bf16[32,8,1024]{2,1,0:T(8,128)(2,1)}), bf16[32,8,1024]{2,1,0:T(8,128)(2,1)S(1)}, u32[]{:S(2)}, u32[]{:S(2)}) async-start(bf16[32,8,1024]{2,1,0:T(8,128)(2,1)} %fusion.88), calls=%async_computation.1 | async-start | bytes 1048576 | tf_op jit(solution)/shard_map/all_to_all | solution.py:133
  12.6 1.0 fusion.143
  13.6 4.6 %fusion.120 = bf16[512,512]{0,1:T(8,128)(2,1)} fusion(), kind=kLoop, calls=%fused_computation.137 | loop fusion | flops 3932160 | bytes 524288 | tf_op jit(solution)/shard_map/cos | solution.py:47
  18.2 4.6 %fusion.119 = bf16[512,512]{0,1:T(8,128)(2,1)} fusion(), kind=kLoop, calls=%fused_computation.136 | loop fusion | flops 3932160 | bytes 524288 | tf_op jit(solution)/shard_map/sin | solution.py:47
  22.8 1.1 fusion.89
  24.1 7.2 %all-to-all-start.3 = ((bf16[32,8,1024]{2,1,0:T(8,128)(2,1)}), bf16[32,8,1024]{2,1,0:T(8,128)(2,1)}, u32[]{:S(2)}, u32[]{:S(2)}) async-start(bf16[32,8,1024]{2,1,0:T(8,128)(2,1)} %fusion.89), calls=%async_computation.3 | async-start | bytes 1048576 | tf_op jit(solution)/shard_map/all_to_all | solution.py:132
  31.7 1.0 reshape.97
  32.7 1.6 fusion.122
  34.3 1.8 fusion.125
  36.1 6.9 %all-to-all-done.3 = bf16[32,8,1024]{2,1,0:T(8,128)(2,1)} async-done(((bf16[32,8,1024]{2,1,0:T(8,128)(2,1)}), bf16[32,8,1024]{2,1,0:T(8,128)(2,1)}, u32[]{:S(2)}, u32[]{:S(2)}) %all-to-all-start.3) | async-done | bytes 524320 | tf_op jit(solution)/shard_map/all_to_all | solution.py:132
  43.0 0.8 broadcast_in_dim.6
  43.8 8.2 %all-to-all-start = ((bf16[8,8,4096]{2,1,0:T(8,128)(2,1)}), bf16[8,8,4096]{2,1,0:T(8,128)(2,1)}, u32[]{:S(2)}, u32[]{:S(2)}) async-start(bf16[8,8,4096]{2,1,0:T(8,128)(2,1)} %broadcast_in_dim.6), calls=%async_computation | async-start | bytes 1048576 | tf_op jit(solution)/shard_map/all_to_all | solution.py:20
  52.0 2.1 %copy.144 = bf16[8,32,1024]{2,1,0:T(8,128)(2,1)} copy(bf16[8,32,1024]{2,0,1:T(8,128)(2,1)} %bitcast.24) | data formatting | bytes 1048576 | tf_op jit(solution)/shard_map/all_to_all | solution.py:132
  54.1 2.1 %reshape.98 = bf16[8,256,128]{2,1,0:T(8,128)(2,1)} reshape(bf16[8,32,1024]{2,1,0:T(8,128)(2,1)} %copy.144) | data formatting | bytes 1048576 | tf_op jit(solution)/shard_map/reshape | solution.py:63
  56.2 1.6 fusion.121
  59.0 0.8 fusion.130
  61.4 2.2 %convolution_add_fusion.1 = f32[8,512,128]{2,1,0:T(8,128)} fusion(f32[8,512,128]{2,1,0:T(8,128)S(1)} %fusion.127, f32[8,128,512]{1,2,0:T(8,128)S(1)} %fusion.122, f32[8,128,512]{1,2,0:T(8,128)S(1)} %copy-done.2, f32[128,512]{0,1:T(8,128)S(1)} %get-tuple-element.28, f32[128,512]{0,1:T(8,128)S(1)} %get-tuple-element.29), kind=kOutput, calls=%fused_computation.74 | convolution fusion | flops 137068544 | bytes 8912896 | tf_op jit(solution)/shard_map/fk,ckg->cfg/dot_general | solution.py:76
  63.6 2.1 %fusion.128 = f32[8,512,128]{2,1,0:T(8,128)} fusion(f32[8,128,512]{1,2,0:T(8,128)S(1)} %fusion.122, f32[8,128,512]{1,2,0:T(8,128)S(1)} %copy-done.2, f32[128,512]{0,1:T(8,128)S(1)} %get-tuple-element.28, f32[128,512]{0,1:T(8,128)S(1)} %get-tuple-element.29), kind=kOutput, calls=%fused_computation.148 | convolution fusion | flops 136544256 | bytes 6815744 | tf_op jit(solution)/shard_map/fk,ckg->cfg/dot_general | solution.py:77
  65.8 2.3 %convolution_add_fusion = f32[8,512,128]{2,1,0:T(8,128)} fusion(f32[8,512,128]{2,1,0:T(8,128)S(1)} %fusion.129, f32[8,128,512]{1,2,0:T(8,128)S(1)} %fusion.121, f32[8,128,512]{1,2,0:T(8,128)S(1)} %fusion.124, f32[128,512]{0,1:T(8,128)S(1)} %get-tuple-element.28, f32[128,512]{0,1:T(8,128)S(1)} %get-tuple-element.29), kind=kOutput, calls=%fused_computation.71 | convolution fusion | flops 137068544 | bytes 8912896 | tf_op jit(solution)/shard_map/fk,ckg->cfg/dot_general | solution.py:76
  68.0 2.2 %convolution_subtract_fusion = f32[8,512,128]{2,1,0:T(8,128)} fusion(f32[8,512,128]{2,1,0:T(8,128)S(1)} %fusion.130, f32[8,128,512]{1,2,0:T(8,128)S(1)} %fusion.121, f32[8,128,512]{1,2,0:T(8,128)S(1)} %fusion.124, f32[128,512]{0,1:T(8,128)S(1)} %get-tuple-element.28, f32[128,512]{0,1:T(8,128)S(1)} %get-tuple-element.29), kind=kOutput, calls=%fused_computation.70 | convolution fusion | flops 137068544 | bytes 8912896 | tf_op jit(solution)/shard_map/fk,ckg->cfg/dot_general | solution.py:78
  70.3 2.1 %copy.132 = bf16[8,8,4096]{2,1,0:T(8,128)(2,1)} copy(bf16[8,8,4096]{2,0,1:T(8,128)(2,1)} %bitcast.2) | data formatting | bytes 1048576 | tf_op jit(solution)/shard_map/transpose | solution.py:15
  72.4 2.1 %reshape.96 = bf16[8,256,128]{2,1,0:T(8,128)(2,1)} reshape(bf16[8,8,4096]{2,1,0:T(8,128)(2,1)} %copy.132) | data formatting | bytes 1048576 | tf_op jit(solution)/shard_map/reshape | solution.py:63
  74.5 1.6 fusion.123
  78.2 0.9 convolution_add_fusion.2
  79.1 0.9 convolution_subtract_fusion.2
  80.0 0.8 copy-done.3
  82.6 3.8 %multiply_add_fusion = (bf16[8,512,128]{2,1,0:T(8,128)(2,1)S(1)}, bf16[8,512,128]{2,1,0:T(8,128)(2,1)S(1)}, bf16[8,512,128]{2,1,0:T(8,128)(2,1)S(1)}, bf16[8,512...) fusion(f32[8,512,128]{2,1,0:T(8,128)S(1)} %copy-done.9, ...), kind=kOutput, calls=%fused_computation.55 | convolution fusion | flops 149651456 | bytes 23592960 | tf_op jit(solution)/shard_map/fk,ckg->cfg/dot_general | solution.py:78
  87.7 2.1 %fusion.36 = f32[8,512,128]{2,1,0:T(8,128)} fusion(bf16[8,512,128]{2,1,0:T(8,128)(2,1)S(1)} %get-tuple-element.22), kind=kOutput, calls=%fused_computation.42 | convolution fusion | flops 134447104 | bytes 3145728 | tf_op jit(solution)/shard_map/tf,cfg->ctg/dot_general | solution.py:90
  89.8 2.0 %fusion.34 = f32[8,512,128]{2,1,0:T(8,128)} fusion(bf16[8,512,128]{2,1,0:T(8,128)(2,1)S(1)} %get-tuple-element.22), kind=kOutput, calls=%fused_computation.40 | convolution fusion | flops 134447104 | bytes 3145728 | tf_op jit(solution)/shard_map/tf,cfg->ctg/dot_general | solution.py:91
  91.8 2.0 %fusion.22 = f32[8,512,128]{2,1,0:T(8,128)} fusion(bf16[8,512,128]{2,1,0:T(8,128)(2,1)S(1)} %get-tuple-element.20), kind=kOutput, calls=%fused_computation.26 | convolution fusion | flops 134447104 | bytes 3145728 | tf_op jit(solution)/shard_map/tf,cfg->ctg/dot_general | solution.py:90
  93.8 2.0 %fusion.20 = f32[8,512,128]{2,1,0:T(8,128)} fusion(bf16[8,512,128]{2,1,0:T(8,128)(2,1)S(1)} %get-tuple-element.20), kind=kOutput, calls=%fused_computation.24 | convolution fusion | flops 134447104 | bytes 3145728 | tf_op jit(solution)/shard_map/tf,cfg->ctg/dot_general | solution.py:91
  98.1 2.1 %multiply_reduce_fusion = (f32[]{:T(128)}, f32[256,8,128]{2,0,1:T(8,128)}) fusion(f32[256,8,128]{2,0,1:T(8,128)S(1)} %fusion.1, f32[8,512,128]{2,1,0:T(8,128)S(1)} %fusion.59, f32[8,512,128]{2,1,0:T(8,128)S(1)} %fusion.56, f32[128,512]{0,1:T(8,128)S(1)} %get-tuple-element.28, f32[128,512]{0,1:T(8,128)S(1)} %get-tuple-element.29, ...), kind=kOutput, calls=%fused_computation.108 | convolution fusion | flops 271056896 | bytes 7077892 | tf_op jit(solution)/shard_map/ckg,gt->ctk/dot_general | solution.py:98
  100.2 1.3 broadcast_in_dim.8
  101.5 3.9 %all-to-all-start.5 = ((f32[32,1,1]{2,1,0:T(1,128)}), f32[32,1,1]{2,1,0:T(1,128)S(1)}, u32[]{:S(2)}, u32[]{:S(2)}) async-start(f32[32,1,1]{2,1,0:T(1,128)} %broadcast_in_dim.8), calls=%async_computation.5 | async-start | bytes 32768 | tf_op jit(solution)/shard_map/all_to_all | solution.py:20
  105.4 2.4 %fusion.44 = f32[8,512,128]{2,1,0:T(8,128)S(1)} fusion(f32[8,512,128]{2,1,0:T(8,128)} %fusion.36, bf16[8,512,128]{2,1,0:T(8,128)(2,1)S(1)} %copy-done.5), kind=kOutput, calls=%fused_computation.64 | convolution fusion | flops 134971392 | bytes 5242880 | tf_op jit(solution)/shard_map/tf,cfg->ctg/dot_general | solution.py:89
  109.0 1.6 fusion.68
  110.6 2.5 %mul.883 = f32[8,32,1024]{2,1,0:T(8,128)} reshape(f32[8,256,128]{2,1,0:T(8,128)} %fusion.68) | data formatting | bytes 2097152 | tf_op jit(solution)/shard_map/mul | solution.py:100
  113.1 2.4 %fusion.50 = f32[8,512,128]{2,1,0:T(8,128)S(1)} fusion(f32[8,512,128]{2,1,0:T(8,128)} %fusion.22, bf16[8,512,128]{2,1,0:T(8,128)(2,1)S(1)} %copy-done.4), kind=kOutput, calls=%fused_computation.66 | convolution fusion | flops 134971392 | bytes 5242880 | tf_op jit(solution)/shard_map/tf,cfg->ctg/dot_general | solution.py:89
  117.3 1.2 mul.900
  119.0 3.4 %fusion.94 = (bf16[8,32,1024]{2,0,1:T(8,128)(2,1)}, bf16[8,32,1024]{2,0,1:T(8,128)(2,1)S(1)}) fusion(f32[8,32,1024]{2,1,0:T(8,128)} %mul.900, f32[8]{0:T(128)S(1)} %copy-done.25, bf16[32,8,1024]{2,1,0:T(8,128)(2,1)} %all-to-all-done.3, bf16[32,8,1024]{2,1,0:T(8,128)(2,1)S(1)} %copy-done.15, f32[8,32,1024]{2,1,0:T(8,128)S(1)} %copy-done.20), kind=kLoop, calls=%fused_computation.103 | loop fusion | flops 2097152 | bytes 4194336 | tf_op jit(solution)/shard_map/convert_element_type | solution.py:146
  122.4 18.9 %all_to_all.74 = bf16[8,32,1024]{2,0,1:T(8,128)(2,1)S(1)} all-to-all(bf16[8,32,1024]{2,0,1:T(8,128)(2,1)S(1)} %get-tuple-element.25), channel_id=1, replica_groups=mesh['ex'=8,'ctx'=32] {'ctx'}, dimensions={1} | all-to-all | bytes 1048576 | tf_op jit(solution)/shard_map/all_to_all | solution.py:161
  141.4 3.7 %all-to-all-start.4 = ((bf16[8,32,1024]{2,0,1:T(8,128)(2,1)}), bf16[8,32,1024]{2,0,1:T(8,128)(2,1)S(1)}, u32[]{:S(2)}, u32[]{:S(2)}) async-start(bf16[8,32,1024]{2,0,1:T(8,128)(2,1)} %get-tuple-element.24), calls=%async_computation.4 | async-start | bytes 1048576 | tf_op jit(solution)/shard_map/all_to_all | solution.py:162
  147.4 1.1 copy.190
  148.5 8.1 %all-to-all-done.4 = bf16[8,32,1024]{2,0,1:T(8,128)(2,1)S(1)} async-done(((bf16[8,32,1024]{2,0,1:T(8,128)(2,1)}), bf16[8,32,1024]{2,0,1:T(8,128)(2,1)S(1)}, u32[]{:S(2)}, u32[]{:S(2)}) %all-to-all-start.4) | async-done | bytes 524320 | tf_op jit(solution)/shard_map/all_to_all | solution.py:162
  156.6 6.9 %all-to-all-start.6 = ((bf16[8,8,4096]{2,1,0:T(8,128)(2,1)}), bf16[8,8,4096]{2,1,0:T(8,128)(2,1)S(1)}, u32[]{:S(2)}, u32[]{:S(2)}) async-start(bf16[8,8,4096]{2,1,0:T(8,128)(2,1)} %bitcast.285), calls=%async_computation.6 | async-start | bytes 1048576 | tf_op jit(solution)/shard_map/all_to_all | solution.py:38
  164.3 1.0 copy.159
  165.3 16.3 %all-to-all-done.6 = bf16[8,8,4096]{2,1,0:T(8,128)(2,1)S(1)} async-done(((bf16[8,8,4096]{2,1,0:T(8,128)(2,1)}), bf16[8,8,4096]{2,1,0:T(8,128)(2,1)S(1)}, u32[]{:S(2)}, u32[]{:S(2)}) %all-to-all-start.6) | async-done | bytes 524320 | tf_op jit(solution)/shard_map/all_to_all | solution.py:38
  (79 shorter events, 17.8 us)
Async XLA Ops:
  0.6 1.1 copy-start
  0.6 11.9 %copy-start.24 = (f32[8,4096]{1,0:T(8,128)S(1)}, f32[8,4096]{1,0:T(8,128)}, u32[]{:S(2)}) copy-start(f32[8,4096]{1,0:T(8,128)} %param.14) | copy-start | bytes 393220
  1.7 21.1 %copy-start.22 = (bf16[256,256]{1,0:T(8,128)(2,1)S(1)}, bf16[256,256]{1,0:T(8,128)(2,1)}, u32[]{:S(2)}) copy-start(bf16[256,256]{1,0:T(8,128)(2,1)} %param.12) | copy-start | bytes 393220
  4.0 20.2 %all-to-all-start.1 = ((bf16[32,8,1024]{2,1,0:T(8,128)(2,1)}), bf16[32,8,1024]{2,1,0:T(8,128)(2,1)S(1)}, u32[]{:S(2)}, u32[]{:S(2)}) async-start(bf16[32,8,1024]{2,1,0:T(8,128)(2,1)} %fusion.88), calls=%async_computation.1 | async-start | bytes 1048576 | tf_op jit(solution)/shard_map/all_to_all | solution.py:133
  24.1 7.5 %copy-start.14 = (bf16[32,8,1024]{2,1,0:T(8,128)(2,1)}, bf16[32,8,1024]{2,1,0:T(8,128)(2,1)S(1)}, u32[]{:S(2)}) copy-start(bf16[32,8,1024]{2,1,0:T(8,128)(2,1)S(1)} %all-to-all-done.1) | copy-start | bytes 1572868
  24.1 18.8 %all-to-all-start.3 = ((bf16[32,8,1024]{2,1,0:T(8,128)(2,1)}), bf16[32,8,1024]{2,1,0:T(8,128)(2,1)}, u32[]{:S(2)}, u32[]{:S(2)}) async-start(bf16[32,8,1024]{2,1,0:T(8,128)(2,1)} %fusion.89), calls=%async_computation.3 | async-start | bytes 1048576 | tf_op jit(solution)/shard_map/all_to_all | solution.py:132
  31.6 2.7 %copy-start.6 = (bf16[512,512]{0,1:T(8,128)(2,1)S(1)}, bf16[512,512]{0,1:T(8,128)(2,1)}, u32[]{:S(2)}) copy-start(bf16[512,512]{0,1:T(8,128)(2,1)} %fusion.119) | copy-start | bytes 1572868
  32.7 1.6 copy-start.16
  43.8 26.5 %all-to-all-start = ((bf16[8,8,4096]{2,1,0:T(8,128)(2,1)}), bf16[8,8,4096]{2,1,0:T(8,128)(2,1)}, u32[]{:S(2)}, u32[]{:S(2)}) async-start(bf16[8,8,4096]{2,1,0:T(8,128)(2,1)} %broadcast_in_dim.6), calls=%async_computation | async-start | bytes 1048576 | tf_op jit(solution)/shard_map/all_to_all | solution.py:20
  56.2 1.6 copy-start.17
  59.0 1.6 copy-start.2
  74.5 1.6 copy-start.18
  78.2 1.8 %copy-start.10 = (f32[8,512,128]{2,1,0:T(8,128)S(1)}, f32[8,512,128]{2,1,0:T(8,128)}, u32[]{:S(2)}) copy-start(f32[8,512,128]{2,1,0:T(8,128)} %fusion.128) | copy-start | bytes 6291460
  79.1 1.8 copy-start.3
  79.1 2.4 %copy-start.7 = (f32[8,512,128]{2,1,0:T(8,128)S(1)}, f32[8,512,128]{2,1,0:T(8,128)}, u32[]{:S(2)}) copy-start(f32[8,512,128]{2,1,0:T(8,128)} %convolution_add_fusion.1) | copy-start | bytes 6291460
  79.1 3.0 %copy-start.8 = (f32[8,512,128]{2,1,0:T(8,128)S(1)}, f32[8,512,128]{2,1,0:T(8,128)}, u32[]{:S(2)}) copy-start(f32[8,512,128]{2,1,0:T(8,128)} %convolution_add_fusion) | copy-start | bytes 6291460
  79.1 3.6 %copy-start.9 = (f32[8,512,128]{2,1,0:T(8,128)S(1)}, f32[8,512,128]{2,1,0:T(8,128)}, u32[]{:S(2)}) copy-start(f32[8,512,128]{2,1,0:T(8,128)} %convolution_subtract_fusion) | copy-start | bytes 6291460
  96.5 1.0 copy-start.13
  98.0 7.3 %copy-start.5 = (bf16[8,512,128]{2,1,0:T(8,128)(2,1)S(1)}, bf16[8,512,128]{2,1,0:T(8,128)(2,1)}, u32[]{:S(2)}) copy-start(bf16[8,512,128]{2,1,0:T(8,128)(2,1)} %get-tuple-element.23) | copy-start | bytes 3145732
  101.5 21.0 %all-to-all-start.5 = ((f32[32,1,1]{2,1,0:T(1,128)}), f32[32,1,1]{2,1,0:T(1,128)S(1)}, u32[]{:S(2)}, u32[]{:S(2)}) async-start(f32[32,1,1]{2,1,0:T(1,128)} %broadcast_in_dim.8), calls=%async_computation.5 | async-start | bytes 32768 | tf_op jit(solution)/shard_map/all_to_all | solution.py:20
  105.4 2.4 %copy-start.12 = (f32[8,512,128]{2,1,0:T(8,128)S(1)}, f32[8,512,128]{2,1,0:T(8,128)}, u32[]{:S(2)}) copy-start(f32[8,512,128]{2,1,0:T(8,128)} %fusion.34) | copy-start | bytes 6291460
  110.6 2.5 %copy-start.4 = (bf16[8,512,128]{2,1,0:T(8,128)(2,1)S(1)}, bf16[8,512,128]{2,1,0:T(8,128)(2,1)}, u32[]{:S(2)}) copy-start(bf16[8,512,128]{2,1,0:T(8,128)(2,1)} %get-tuple-element.21) | copy-start | bytes 3145732
  113.1 2.4 %copy-start.11 = (f32[8,512,128]{2,1,0:T(8,128)S(1)}, f32[8,512,128]{2,1,0:T(8,128)}, u32[]{:S(2)}) copy-start(f32[8,512,128]{2,1,0:T(8,128)} %fusion.20) | copy-start | bytes 6291460
  117.3 1.2 copy-start.15
  117.3 1.8 copy-start.20
  117.3 1.8 copy-start.25
  122.4 24.6 %copy-start.19 = (f32[256,8,128]{2,0,1:T(8,128)S(1)}, f32[256,8,128]{2,0,1:T(8,128)}, u32[]{:S(2)}) copy-start(f32[256,8,128]{2,0,1:T(8,128)} %get-tuple-element.27) | copy-start | bytes 3145732
  141.4 15.2 %all-to-all-start.4 = ((bf16[8,32,1024]{2,0,1:T(8,128)(2,1)}), bf16[8,32,1024]{2,0,1:T(8,128)(2,1)S(1)}, u32[]{:S(2)}, u32[]{:S(2)}) async-start(bf16[8,32,1024]{2,0,1:T(8,128)(2,1)} %get-tuple-element.24), calls=%async_computation.4 | async-start | bytes 1048576 | tf_op jit(solution)/shard_map/all_to_all | solution.py:162
  147.4 16.4 %copy-start.21 = (bf16[1,256,1024]{2,1,0:T(8,128)(2,1)S(1)}, bf16[1,256,1024]{2,1,0:T(8,128)(2,1)}, u32[]{:S(2)}) copy-start(bf16[1,256,1024]{2,1,0:T(8,128)(2,1)} %param.9) | copy-start | bytes 1572868
  147.4 16.4 %copy-start.23 = (bf16[256,256]{1,0:T(8,128)(2,1)S(1)}, bf16[256,256]{1,0:T(8,128)(2,1)}, u32[]{:S(2)}) copy-start(bf16[256,256]{1,0:T(8,128)(2,1)} %param.13) | copy-start | bytes 393220
  156.6 25.0 %all-to-all-start.6 = ((bf16[8,8,4096]{2,1,0:T(8,128)(2,1)}), bf16[8,8,4096]{2,1,0:T(8,128)(2,1)S(1)}, u32[]{:S(2)}, u32[]{:S(2)}) async-start(bf16[8,8,4096]{2,1,0:T(8,128)(2,1)} %bitcast.285), calls=%async_computation.6 | async-start | bytes 1048576 | tf_op jit(solution)/shard_map/all_to_all | solution.py:38
  163.5 18.8 %copy-start.1 = (bf16[1,256,1024]{2,1,0:T(8,128)(2,1)S(1)}, bf16[1,256,1024]{2,1,0:T(8,128)(2,1)}, u32[]{:S(2)}) copy-start(bf16[1,256,1024]{2,1,0:T(8,128)(2,1)} %param.8) | copy-start | bytes 1572868
where the time goes:
time: 183 us; the launch traced here: 182 us
  matrix products  52.6 us (29%)
  starting transfers between devices  38.5 us (21%)
  waiting for transfers between devices  31.5 us (17%)
  local copies, waits for them, and re-layouts  22.5 us (12%)
  blocking collectives  18.9 us (10%)
  other arithmetic  15.9 us (9%)
  between operations  2.43 us (1%)
    all_to_all x1, blocking collectives, on_device(): lax.all_to_all(value_grad_ch, 'ctx', split_axis=1, concat_axis=0, tiled=T...  18.9 us
    all_to_all x1, waiting for transfers between devices, sum_at_owner(): parts = lax.all_to_all(cut_along(x, dim, size), axis, 0, 0, tiled=True)  16.3 us
    all_to_all x2, starting transfers between devices, from_everyone(): return lax.all_to_all(copies, axis, split_axis=0, concat_axis=0, tiled=True)  12.1 us
    all_to_all x1, starting transfers between devices, on_device(): lax.all_to_all(signal_tok, 'ctx', split_axis=0, concat_axis=1, tiled=True)  8.58 us
    all_to_all x1, waiting for transfers between devices, on_device(): lax.all_to_all(conv_state, 'ctx', split_axis=1, concat_axis=0, tiled=True)  8.05 us
    all_to_all x1, starting transfers between devices, on_device(): lax.all_to_all(value_tok, 'ctx', split_axis=0, concat_axis=1, tiled=True)  7.19 us
    all_to_all x1, starting transfers between devices, sum_at_owner(): parts = lax.all_to_all(cut_along(x, dim, size), axis, 0, 0, tiled=True)  6.92 us
    dot_general x3, matrix products, second_section(): out_imag = out_imag - jnp.einsum('fk,ckg->cfg', sin_short, twist_real)  6.9 us
  transfers between devices with their start and end apart: 6, of which 4 were waited for; matrix products, arithmetic and copies ran while one was open for 29% of the time, Pallas kernels for 0%

commit v1 on v0

--- a/solution.py
+++ b/solution.py
@@ -158,7 +158,12 @@
         half_blocks,
     )
     value_grad_tok, state_tok = (
-        lax.all_to_all(value_grad_ch, "ctx", split_axis=1, concat_axis=0, tiled=True),
+        jnp.concatenate(
+            lax.all_to_all(
+                jnp.stack(jnp.split(value_grad_ch, lax.axis_size("ctx"), axis=1)), "ctx", 0, 0
+            ),
+            axis=0,
+        ),
         lax.all_to_all(conv_state, "ctx", split_axis=1, concat_axis=0, tiled=True),
     )
     gate_grad_tok = (state_tok.astype(jnp.float32) * cot_tok).astype(jnp.bfloat16)

time: 183 us -> 200 us (1.093)
  blocking collectives: 18.9 us -> 0 us
  local copies, waits for them, and re-layouts: 22.5 us -> 40.7 us
  waiting for transfers between devices: 31.5 us -> 41.3 us
  starting transfers between devices: 38.5 us -> 45.9 us
    all_to_all x1 -> x0, blocking collectives: 18.9 us -> none  [on_device(): lax.all_to_all(value_grad_ch, 'ctx', split_axis=1, concat_axis=0, tiled=T...]
    unnamed x53 -> x84, local copies, waits for them, and re-layouts: 5.75 us -> 24.4 us
    all_to_all x0 -> x1, waiting for transfers between devices: none -> 8.11 us  [on_device(): lax.all_to_all(jnp.stack(jnp.split(value_grad_ch, lax.axis_size('ctx'), a...]
    all_to_all x1, starting transfers between devices: 3.68 us -> 7.39 us  [on_device(): lax.all_to_all(conv_state, 'ctx', split_axis=1, concat_axis=0, tiled=True)]
    all_to_all x0 -> x1, starting transfers between devices: none -> 3.68 us  [on_device(): lax.all_to_all(jnp.stack(jnp.split(value_grad_ch, lax.axis_size('ctx'), a...]
  transfers between devices with their start and end apart: 6 -> 7, of which waited for: 4 -> 5; matrix products, arithmetic and copies ran while one was open for 29% -> 36% of each run, Pallas kernels for 0% -> 0%
where the time goes in v1:
time: 200 us; the launch traced here: 199 us
  matrix products  52.7 us (26%)
  starting transfers between devices  45.9 us (23%)
  waiting for transfers between devices  41.3 us (21%)
  local copies, waits for them, and re-layouts  40.7 us (20%)
  other arithmetic  15.6 us (8%)
  between operations  2.43 us (1%)
    unnamed x84, local copies, waits for them, and re-layouts  24.4 us
    all_to_all x1, waiting for transfers between devices, sum_at_owner(): parts = lax.all_to_all(cut_along(x, dim, size), axis, 0, 0, tiled=True)  16.3 us
    all_to_all x2, starting transfers between devices, from_everyone(): return lax.all_to_all(copies, axis, split_axis=0, concat_axis=0, tiled=True)  12.1 us
    all_to_all x1, waiting for transfers between devices, on_device(): lax.all_to_all(conv_state, 'ctx', split_axis=1, concat_axis=0, tiled=True)  9.77 us
    all_to_all x1, starting transfers between devices, on_device(): lax.all_to_all(signal_tok, 'ctx', split_axis=0, concat_axis=1, tiled=True)  8.58 us
    all_to_all x1, waiting for transfers between devices, on_device(): lax.all_to_all(jnp.stack(jnp.split(value_grad_ch, lax.axis_size('ctx'), a...  8.11 us
    all_to_all x1, starting transfers between devices, on_device(): lax.all_to_all(conv_state, 'ctx', split_axis=1, concat_axis=0, tiled=True)  7.39 us
    all_to_all x1, starting transfers between devices, on_device(): lax.all_to_all(value_tok, 'ctx', split_axis=0, concat_axis=1, tiled=True)  7.21 us
  transfers between devices with their start and end apart: 7, of which 5 were waited for; matrix products, arithmetic and copies ran while one was open for 36% of the time, Pallas kernels for 0%

profile of v1, /device:TPU:1, one launch (start us, length us, event | category | flops | bytes accessed | tf_op | source)
XLA Modules:
  0.0 198.5 jit_solution(15319207876102332047)
XLA Ops:
  1.7 2.2 %fusion.88 = bf16[32,8,1024]{2,1,0:T(8,128)(2,1)} fusion(bf16[256,256]{1,0:T(8,128)(2,1)} %param.13, bf16[1,256,1024]{2,1,0:T(8,128)(2,1)} %param.9, bf16[1,256,1024]{2,1,0:T(8,128)(2,1)S(1)} %copy-done, f32[1024]{0:T(1024)S(1)} %bitcast.421), kind=kOutput, calls=%fused_computation.94 | convolution fusion | flops 135790592 | bytes 1708032 | tf_op jit(solution)/shard_map/dot_general | solution.py:106
  3.9 8.6 %all-to-all-start.1 = ((bf16[32,8,1024]{2,1,0:T(8,128)(2,1)}), bf16[32,8,1024]{2,1,0:T(8,128)(2,1)S(1)}, u32[]{:S(2)}, u32[]{:S(2)}) async-start(bf16[32,8,1024]{2,1,0:T(8,128)(2,1)} %fusion.88), calls=%async_computation.1 | async-start | bytes 1048576 | tf_op jit(solution)/shard_map/all_to_all | solution.py:133
  12.6 1.0 fusion.143
  13.6 4.6 %fusion.120 = bf16[512,512]{0,1:T(8,128)(2,1)} fusion(), kind=kLoop, calls=%fused_computation.138 | loop fusion | flops 3932160 | bytes 524288 | tf_op jit(solution)/shard_map/cos | solution.py:47
  18.2 4.6 %fusion.119 = bf16[512,512]{0,1:T(8,128)(2,1)} fusion(), kind=kLoop, calls=%fused_computation.137 | loop fusion | flops 3932160 | bytes 524288 | tf_op jit(solution)/shard_map/sin | solution.py:47
  22.8 1.1 fusion.89
  24.1 7.2 %all-to-all-start.3 = ((bf16[32,8,1024]{2,1,0:T(8,128)(2,1)}), bf16[32,8,1024]{2,1,0:T(8,128)(2,1)}, u32[]{:S(2)}, u32[]{:S(2)}) async-start(bf16[32,8,1024]{2,1,0:T(8,128)(2,1)} %fusion.89), calls=%async_computation.3 | async-start | bytes 1048576 | tf_op jit(solution)/shard_map/all_to_all | solution.py:132
  31.7 1.0 reshape.93
  32.7 1.6 fusion.122
  34.3 1.8 fusion.125
  36.1 6.9 %all-to-all-done.3 = bf16[32,8,1024]{2,1,0:T(8,128)(2,1)} async-done(((bf16[32,8,1024]{2,1,0:T(8,128)(2,1)}), bf16[32,8,1024]{2,1,0:T(8,128)(2,1)}, u32[]{:S(2)}, u32[]{:S(2)}) %all-to-all-start.3) | async-done | bytes 524320 | tf_op jit(solution)/shard_map/all_to_all | solution.py:132
  43.0 0.8 broadcast_in_dim.6
  43.8 8.2 %all-to-all-start = ((bf16[8,8,4096]{2,1,0:T(8,128)(2,1)}), bf16[8,8,4096]{2,1,0:T(8,128)(2,1)}, u32[]{:S(2)}, u32[]{:S(2)}) async-start(bf16[8,8,4096]{2,1,0:T(8,128)(2,1)} %broadcast_in_dim.6), calls=%async_computation | async-start | bytes 1048576 | tf_op jit(solution)/shard_map/all_to_all | solution.py:20
  52.0 2.1 %copy.115 = bf16[8,32,1024]{2,1,0:T(8,128)(2,1)} copy(bf16[8,32,1024]{2,0,1:T(8,128)(2,1)} %bitcast.56) | data formatting | bytes 1048576 | tf_op jit(solution)/shard_map/all_to_all | solution.py:132
  54.1 2.1 %reshape.95 = bf16[8,256,128]{2,1,0:T(8,128)(2,1)} reshape(bf16[8,32,1024]{2,1,0:T(8,128)(2,1)} %copy.115) | data formatting | bytes 1048576 | tf_op jit(solution)/shard_map/reshape | solution.py:63
  56.2 1.6 fusion.121
  59.1 0.8 fusion.130
  61.4 2.2 %convolution_add_fusion.1 = f32[8,512,128]{2,1,0:T(8,128)} fusion(f32[8,512,128]{2,1,0:T(8,128)S(1)} %fusion.127, f32[8,128,512]{1,2,0:T(8,128)S(1)} %fusion.122, f32[8,128,512]{1,2,0:T(8,128)S(1)} %copy-done.2, f32[128,512]{0,1:T(8,128)S(1)} %get-tuple-element.24, f32[128,512]{0,1:T(8,128)S(1)} %get-tuple-element.25), kind=kOutput, calls=%fused_computation.74 | convolution fusion | flops 137068544 | bytes 8912896 | tf_op jit(solution)/shard_map/fk,ckg->cfg/dot_general | solution.py:76
  63.7 2.1 %fusion.128 = f32[8,512,128]{2,1,0:T(8,128)} fusion(f32[8,128,512]{1,2,0:T(8,128)S(1)} %fusion.122, f32[8,128,512]{1,2,0:T(8,128)S(1)} %copy-done.2, f32[128,512]{0,1:T(8,128)S(1)} %get-tuple-element.24, f32[128,512]{0,1:T(8,128)S(1)} %get-tuple-element.25), kind=kOutput, calls=%fused_computation.149 | convolution fusion | flops 136544256 | bytes 6815744 | tf_op jit(solution)/shard_map/fk,ckg->cfg/dot_general | solution.py:77
  65.8 2.3 %convolution_add_fusion = f32[8,512,128]{2,1,0:T(8,128)} fusion(f32[8,512,128]{2,1,0:T(8,128)S(1)} %fusion.129, f32[8,128,512]{1,2,0:T(8,128)S(1)} %fusion.121, f32[8,128,512]{1,2,0:T(8,128)S(1)} %fusion.124, f32[128,512]{0,1:T(8,128)S(1)} %get-tuple-element.24, f32[128,512]{0,1:T(8,128)S(1)} %get-tuple-element.25), kind=kOutput, calls=%fused_computation.71 | convolution fusion | flops 137068544 | bytes 8912896 | tf_op jit(solution)/shard_map/fk,ckg->cfg/dot_general | solution.py:76
  68.1 2.2 %convolution_subtract_fusion = f32[8,512,128]{2,1,0:T(8,128)} fusion(f32[8,512,128]{2,1,0:T(8,128)S(1)} %fusion.130, f32[8,128,512]{1,2,0:T(8,128)S(1)} %fusion.121, f32[8,128,512]{1,2,0:T(8,128)S(1)} %fusion.124, f32[128,512]{0,1:T(8,128)S(1)} %get-tuple-element.24, f32[128,512]{0,1:T(8,128)S(1)} %get-tuple-element.25), kind=kOutput, calls=%fused_computation.70 | convolution fusion | flops 137068544 | bytes 8912896 | tf_op jit(solution)/shard_map/fk,ckg->cfg/dot_general | solution.py:78
  70.3 2.1 %copy.104 = bf16[8,8,4096]{2,1,0:T(8,128)(2,1)} copy(bf16[8,8,4096]{2,0,1:T(8,128)(2,1)} %bitcast.2) | data formatting | bytes 1048576 | tf_op jit(solution)/shard_map/transpose | solution.py:15
  72.4 2.1 %reshape.92 = bf16[8,256,128]{2,1,0:T(8,128)(2,1)} reshape(bf16[8,8,4096]{2,1,0:T(8,128)(2,1)} %copy.104) | data formatting | bytes 1048576 | tf_op jit(solution)/shard_map/reshape | solution.py:63
  74.5 1.6 fusion.123
  78.2 0.9 convolution_add_fusion.2
  79.1 0.9 convolution_subtract_fusion.2
  80.0 0.8 copy-done.3
  82.7 3.8 %multiply_add_fusion = (bf16[8,512,128]{2,1,0:T(8,128)(2,1)S(1)}, bf16[8,512,128]{2,1,0:T(8,128)(2,1)S(1)}, bf16[8,512,128]{2,1,0:T(8,128)(2,1)S(1)}, bf16[8,512...) fusion(f32[8,512,128]{2,1,0:T(8,128)S(1)} %copy-done.9, ...), kind=kOutput, calls=%fused_computation.55 | convolution fusion | flops 149651456 | bytes 23592960 | tf_op jit(solution)/shard_map/fk,ckg->cfg/dot_general | solution.py:78
  87.8 2.1 %fusion.22 = f32[8,512,128]{2,1,0:T(8,128)} fusion(bf16[8,512,128]{2,1,0:T(8,128)(2,1)S(1)} %get-tuple-element.18), kind=kOutput, calls=%fused_computation.26 | convolution fusion | flops 134447104 | bytes 3145728 | tf_op jit(solution)/shard_map/tf,cfg->ctg/dot_general | solution.py:90
  89.9 2.0 %fusion.20 = f32[8,512,128]{2,1,0:T(8,128)} fusion(bf16[8,512,128]{2,1,0:T(8,128)(2,1)S(1)} %get-tuple-element.18), kind=kOutput, calls=%fused_computation.24 | convolution fusion | flops 134447104 | bytes 3145728 | tf_op jit(solution)/shard_map/tf,cfg->ctg/dot_general | solution.py:91
  92.0 2.0 %fusion.36 = f32[8,512,128]{2,1,0:T(8,128)} fusion(bf16[8,512,128]{2,1,0:T(8,128)(2,1)S(1)} %get-tuple-element.20), kind=kOutput, calls=%fused_computation.42 | convolution fusion | flops 134447104 | bytes 3145728 | tf_op jit(solution)/shard_map/tf,cfg->ctg/dot_general | solution.py:90
  94.0 2.0 %fusion.34 = f32[8,512,128]{2,1,0:T(8,128)} fusion(bf16[8,512,128]{2,1,0:T(8,128)(2,1)S(1)} %get-tuple-element.20), kind=kOutput, calls=%fused_computation.40 | convolution fusion | flops 134447104 | bytes 3145728 | tf_op jit(solution)/shard_map/tf,cfg->ctg/dot_general | solution.py:91
  98.2 2.1 %multiply_reduce_fusion = (f32[]{:T(128)}, f32[256,8,128]{2,0,1:T(8,128)}) fusion(f32[256,8,128]{2,0,1:T(8,128)S(1)} %fusion.1, f32[8,512,128]{2,1,0:T(8,128)S(1)} %fusion.59, f32[8,512,128]{2,1,0:T(8,128)S(1)} %fusion.56, f32[128,512]{0,1:T(8,128)S(1)} %get-tuple-element.24, f32[128,512]{0,1:T(8,128)S(1)} %get-tuple-element.25, ...), kind=kOutput, calls=%fused_computation.109 | convolution fusion | flops 271056896 | bytes 7077892 | tf_op jit(solution)/shard_map/ckg,gt->ctk/dot_general | solution.py:98
  100.3 1.3 broadcast_in_dim.8
  101.6 3.9 %all-to-all-start.5 = ((f32[32,1,1]{2,1,0:T(1,128)}), f32[32,1,1]{2,1,0:T(1,128)S(1)}, u32[]{:S(2)}, u32[]{:S(2)}) async-start(f32[32,1,1]{2,1,0:T(1,128)} %broadcast_in_dim.8), calls=%async_computation.5 | async-start | bytes 32768 | tf_op jit(solution)/shard_map/all_to_all | solution.py:20
  105.5 2.4 %fusion.50 = f32[8,512,128]{2,1,0:T(8,128)S(1)} fusion(f32[8,512,128]{2,1,0:T(8,128)} %fusion.22, bf16[8,512,128]{2,1,0:T(8,128)(2,1)S(1)} %copy-done.5), kind=kOutput, calls=%fused_computation.66 | convolution fusion | flops 134971392 | bytes 5242880 | tf_op jit(solution)/shard_map/tf,cfg->ctg/dot_general | solution.py:89
  109.1 1.6 fusion.77
  110.7 2.5 %mul.900 = f32[8,32,1024]{2,1,0:T(8,128)} reshape(f32[8,256,128]{2,1,0:T(8,128)} %fusion.77) | data formatting | bytes 2097152 | tf_op jit(solution)/shard_map/mul | solution.py:100
  113.2 2.4 %fusion.44 = f32[8,512,128]{2,1,0:T(8,128)S(1)} fusion(f32[8,512,128]{2,1,0:T(8,128)} %fusion.36, bf16[8,512,128]{2,1,0:T(8,128)(2,1)S(1)} %copy-done.4), kind=kOutput, calls=%fused_computation.64 | convolution fusion | flops 134971392 | bytes 5242880 | tf_op jit(solution)/shard_map/tf,cfg->ctg/dot_general | solution.py:89
  135.5 2.5 %fusion.95 = bf16[8,32,1024]{2,0,1:T(8,128)(2,1)} fusion(f32[8,32,1024]{2,1,0:T(8,128)S(1)} %copy-done.20, f32[8]{0:T(128)S(1)} %copy-done.25, bf16[32,8,1024]{2,1,0:T(8,128)(2,1)} %all-to-all-done.3), kind=kLoop, calls=%fused_computation.106 | loop fusion | flops 1048576 | bytes 2097184 | tf_op jit(solution)/shard_map/convert_element_type | solution.py:146
  138.6 7.4 %all-to-all-start.4 = ((bf16[8,32,1024]{2,0,1:T(8,128)(2,1)}), bf16[8,32,1024]{2,0,1:T(8,128)(2,1)S(1)}, u32[]{:S(2)}, u32[]{:S(2)}) async-start(bf16[8,32,1024]{2,0,1:T(8,128)(2,1)} %fusion.95), calls=%async_computation.4 | async-start | bytes 1048576 | tf_op jit(solution)/shard_map/all_to_all | solution.py:167
  147.8 9.8 %all-to-all-done.4 = bf16[8,32,1024]{2,0,1:T(8,128)(2,1)S(1)} async-done(((bf16[8,32,1024]{2,0,1:T(8,128)(2,1)}), bf16[8,32,1024]{2,0,1:T(8,128)(2,1)S(1)}, u32[]{:S(2)}, u32[]{:S(2)}) %all-to-all-start.4) | async-done | bytes 524320 | tf_op jit(solution)/shard_map/all_to_all | solution.py:167
  157.6 3.7 %all-to-all-start.2 = ((bf16[32,8,1024]{2,1,0:T(8,128)(2,1)}), bf16[32,8,1024]{2,1,0:T(8,128)(2,1)S(1)}, u32[]{:S(2)}, u32[]{:S(2)}) async-start(bf16[32,8,1024]{2,1,0:T(8,128)(2,1)} %constant_dynamic-update-slice_fusion), calls=%async_computation.2 | async-start | bytes 1048576 | tf_op jit(solution)/shard_map/all_to_all | solution.py:162
  163.6 1.1 copy.160
  164.7 8.1 %all-to-all-done.2 = bf16[32,8,1024]{2,1,0:T(8,128)(2,1)S(1)} async-done(((bf16[32,8,1024]{2,1,0:T(8,128)(2,1)}), bf16[32,8,1024]{2,1,0:T(8,128)(2,1)S(1)}, u32[]{:S(2)}, u32[]{:S(2)}) %all-to-all-start.2) | async-done | bytes 524320 | tf_op jit(solution)/shard_map/all_to_all | solution.py:162
  172.8 6.9 %all-to-all-start.6 = ((bf16[8,8,4096]{2,1,0:T(8,128)(2,1)}), bf16[8,8,4096]{2,1,0:T(8,128)(2,1)S(1)}, u32[]{:S(2)}, u32[]{:S(2)}) async-start(bf16[8,8,4096]{2,1,0:T(8,128)(2,1)} %bitcast.418), calls=%async_computation.6 | async-start | bytes 1048576 | tf_op jit(solution)/shard_map/all_to_all | solution.py:38
  180.5 1.0 copy.130
  181.5 16.3 %all-to-all-done.6 = bf16[8,8,4096]{2,1,0:T(8,128)(2,1)S(1)} async-done(((bf16[8,8,4096]{2,1,0:T(8,128)(2,1)}), bf16[8,8,4096]{2,1,0:T(8,128)(2,1)S(1)}, u32[]{:S(2)}, u32[]{:S(2)}) %all-to-all-start.6) | async-done | bytes 524320 | tf_op jit(solution)/shard_map/all_to_all | solution.py:38
  (112 shorter events, 37.6 us)
Async XLA Ops:
  0.6 1.1 copy-start
  0.6 11.9 %copy-start.24 = (f32[8,4096]{1,0:T(8,128)S(1)}, f32[8,4096]{1,0:T(8,128)}, u32[]{:S(2)}) copy-start(f32[8,4096]{1,0:T(8,128)} %param.14) | copy-start | bytes 393220
  1.7 21.1 %copy-start.22 = (bf16[256,256]{1,0:T(8,128)(2,1)S(1)}, bf16[256,256]{1,0:T(8,128)(2,1)}, u32[]{:S(2)}) copy-start(bf16[256,256]{1,0:T(8,128)(2,1)} %param.12) | copy-start | bytes 393220
  3.9 20.2 %all-to-all-start.1 = ((bf16[32,8,1024]{2,1,0:T(8,128)(2,1)}), bf16[32,8,1024]{2,1,0:T(8,128)(2,1)S(1)}, u32[]{:S(2)}, u32[]{:S(2)}) async-start(bf16[32,8,1024]{2,1,0:T(8,128)(2,1)} %fusion.88), calls=%async_computation.1 | async-start | bytes 1048576 | tf_op jit(solution)/shard_map/all_to_all | solution.py:133
  24.1 7.5 %copy-start.14 = (bf16[32,8,1024]{2,1,0:T(8,128)(2,1)}, bf16[32,8,1024]{2,1,0:T(8,128)(2,1)S(1)}, u32[]{:S(2)}) copy-start(bf16[32,8,1024]{2,1,0:T(8,128)(2,1)S(1)} %all-to-all-done.1) | copy-start | bytes 1572868
  24.1 18.9 %all-to-all-start.3 = ((bf16[32,8,1024]{2,1,0:T(8,128)(2,1)}), bf16[32,8,1024]{2,1,0:T(8,128)(2,1)}, u32[]{:S(2)}, u32[]{:S(2)}) async-start(bf16[32,8,1024]{2,1,0:T(8,128)(2,1)} %fusion.89), calls=%async_computation.3 | async-start | bytes 1048576 | tf_op jit(solution)/shard_map/all_to_all | solution.py:132
  31.7 2.6 %copy-start.6 = (bf16[512,512]{0,1:T(8,128)(2,1)S(1)}, bf16[512,512]{0,1:T(8,128)(2,1)}, u32[]{:S(2)}) copy-start(bf16[512,512]{0,1:T(8,128)(2,1)} %fusion.119) | copy-start | bytes 1572868
  32.7 1.6 copy-start.16
  43.8 26.5 %all-to-all-start = ((bf16[8,8,4096]{2,1,0:T(8,128)(2,1)}), bf16[8,8,4096]{2,1,0:T(8,128)(2,1)}, u32[]{:S(2)}, u32[]{:S(2)}) async-start(bf16[8,8,4096]{2,1,0:T(8,128)(2,1)} %broadcast_in_dim.6), calls=%async_computation | async-start | bytes 1048576 | tf_op jit(solution)/shard_map/all_to_all | solution.py:20
  56.2 1.6 copy-start.17
  59.1 1.6 copy-start.2
  74.5 1.6 copy-start.18
  78.2 1.8 copy-start.10
  79.1 1.8 copy-start.3
  79.1 2.4 %copy-start.7 = (f32[8,512,128]{2,1,0:T(8,128)S(1)}, f32[8,512,128]{2,1,0:T(8,128)}, u32[]{:S(2)}) copy-start(f32[8,512,128]{2,1,0:T(8,128)} %convolution_add_fusion.1) | copy-start | bytes 6291460
  79.1 3.0 %copy-start.8 = (f32[8,512,128]{2,1,0:T(8,128)S(1)}, f32[8,512,128]{2,1,0:T(8,128)}, u32[]{:S(2)}) copy-start(f32[8,512,128]{2,1,0:T(8,128)} %convolution_add_fusion) | copy-start | bytes 6291460
  79.1 3.6 %copy-start.9 = (f32[8,512,128]{2,1,0:T(8,128)S(1)}, f32[8,512,128]{2,1,0:T(8,128)}, u32[]{:S(2)}) copy-start(f32[8,512,128]{2,1,0:T(8,128)} %convolution_subtract_fusion) | copy-start | bytes 6291460
  96.6 1.0 copy-start.13
  98.2 7.3 %copy-start.5 = (bf16[8,512,128]{2,1,0:T(8,128)(2,1)S(1)}, bf16[8,512,128]{2,1,0:T(8,128)(2,1)}, u32[]{:S(2)}) copy-start(bf16[8,512,128]{2,1,0:T(8,128)(2,1)} %get-tuple-element.19) | copy-start | bytes 3145732
  101.6 37.1 %all-to-all-start.5 = ((f32[32,1,1]{2,1,0:T(1,128)}), f32[32,1,1]{2,1,0:T(1,128)S(1)}, u32[]{:S(2)}, u32[]{:S(2)}) async-start(f32[32,1,1]{2,1,0:T(1,128)} %broadcast_in_dim.8), calls=%async_computation.5 | async-start | bytes 32768 | tf_op jit(solution)/shard_map/all_to_all | solution.py:20
  105.5 2.4 %copy-start.12 = (f32[8,512,128]{2,1,0:T(8,128)S(1)}, f32[8,512,128]{2,1,0:T(8,128)}, u32[]{:S(2)}) copy-start(f32[8,512,128]{2,1,0:T(8,128)} %fusion.20) | copy-start | bytes 6291460
  110.7 2.5 %copy-start.4 = (bf16[8,512,128]{2,1,0:T(8,128)(2,1)S(1)}, bf16[8,512,128]{2,1,0:T(8,128)(2,1)}, u32[]{:S(2)}) copy-start(bf16[8,512,128]{2,1,0:T(8,128)(2,1)} %get-tuple-element.21) | copy-start | bytes 3145732
  113.2 2.4 %copy-start.11 = (f32[8,512,128]{2,1,0:T(8,128)S(1)}, f32[8,512,128]{2,1,0:T(8,128)}, u32[]{:S(2)}) copy-start(f32[8,512,128]{2,1,0:T(8,128)} %fusion.34) | copy-start | bytes 6291460
  116.8 1.0 copy-start.15
  116.8 1.0 copy-start.25
  117.4 18.1 %copy-start.20 = (f32[8,32,1024]{2,1,0:T(8,128)S(1)}, f32[8,32,1024]{2,1,0:T(8,128)}, u32[]{:S(2)}) copy-start(f32[8,32,1024]{2,1,0:T(8,128)} %mul.900) | copy-start | bytes 3145732
  135.5 27.8 %copy-start.19 = (f32[256,8,128]{2,0,1:T(8,128)S(1)}, f32[256,8,128]{2,0,1:T(8,128)}, u32[]{:S(2)}) copy-start(f32[256,8,128]{2,0,1:T(8,128)} %get-tuple-element.23) | copy-start | bytes 3145732
  138.6 19.0 %all-to-all-start.4 = ((bf16[8,32,1024]{2,0,1:T(8,128)(2,1)}), bf16[8,32,1024]{2,0,1:T(8,128)(2,1)S(1)}, u32[]{:S(2)}, u32[]{:S(2)}) async-start(bf16[8,32,1024]{2,0,1:T(8,128)(2,1)} %fusion.95), calls=%async_computation.4 | async-start | bytes 1048576 | tf_op jit(solution)/shard_map/all_to_all | solution.py:167
  157.6 15.2 %all-to-all-start.2 = ((bf16[32,8,1024]{2,1,0:T(8,128)(2,1)}), bf16[32,8,1024]{2,1,0:T(8,128)(2,1)S(1)}, u32[]{:S(2)}, u32[]{:S(2)}) async-start(bf16[32,8,1024]{2,1,0:T(8,128)(2,1)} %constant_dynamic-update-slice_fusion), calls=%async_computation.2 | async-start | bytes 1048576 | tf_op jit(solution)/shard_map/all_to_all | solution.py:162
  163.6 16.5 %copy-start.21 = (bf16[1,256,1024]{2,1,0:T(8,128)(2,1)S(1)}, bf16[1,256,1024]{2,1,0:T(8,128)(2,1)}, u32[]{:S(2)}) copy-start(bf16[1,256,1024]{2,1,0:T(8,128)(2,1)} %param.9) | copy-start | bytes 1572868
  163.6 16.5 %copy-start.23 = (bf16[256,256]{1,0:T(8,128)(2,1)S(1)}, bf16[256,256]{1,0:T(8,128)(2,1)}, u32[]{:S(2)}) copy-start(bf16[256,256]{1,0:T(8,128)(2,1)} %param.13) | copy-start | bytes 393220
  172.8 25.0 %all-to-all-start.6 = ((bf16[8,8,4096]{2,1,0:T(8,128)(2,1)}), bf16[8,8,4096]{2,1,0:T(8,128)(2,1)S(1)}, u32[]{:S(2)}, u32[]{:S(2)}) async-start(bf16[8,8,4096]{2,1,0:T(8,128)(2,1)} %bitcast.418), calls=%async_computation.6 | async-start | bytes 1048576 | tf_op jit(solution)/shard_map/all_to_all | solution.py:38
  179.8 18.8 %copy-start.1 = (bf16[1,256,1024]{2,1,0:T(8,128)(2,1)S(1)}, bf16[1,256,1024]{2,1,0:T(8,128)(2,1)}, u32[]{:S(2)}) copy-start(bf16[1,256,1024]{2,1,0:T(8,128)(2,1)} %param.8) | copy-start | bytes 1572868
